TPU v7x, 32 devices: a whole 2x2x4 slice. The times are simulated.
32 devices in a mesh: blk: 8 (over z, y), chan: 4 (over x, core).
Axes of the slice: x: 2, y: 2, z: 4, core: 2. Of those that a mesh axis runs over, the one named last changes fastest.
Arguments:
- pair_map: int32 [16, 2], P('blk'), may hold values from 0 to 15, as said below
- visibilities: bfloat16 [2, 16, 64, 1024], P(None, 'blk', 'chan'), may hold values from -24 to 24
- model_vis: bfloat16 [2, 16, 64, 1024], P(None, 'blk', 'chan'), may hold values from -7.2 to 7.2
- flag_mask: int32 [16, 64, 1024], P('blk', 'chan'), may hold values 0 or 1
- gain_amp: float32 [512], replicated, may hold values from 0.19 to 3.17
- gain_phase: float32 [512], replicated, may hold values from -3.1416 to 3.1416
- row_index: int32 [4, 8, 8, 256], P('chan', 'blk'), may hold values from -1 to 32767, as said below
- cell_codes: int32 [2, 4, 8, 8, 256], P(None, 'chan', 'blk'), may hold values from 32 to 992
Outputs:
- grid_tiles: float32 [4, 8, 2, 128, 128], P('chan', 'blk')
- solved_gains: float32 [2, 512], replicated
Inputs may be any that keep to these rules, and one draw needn't show every extreme that they name: `pair_map`: each row is a pair (p, q) of station blocks with p <= q; no two rows are the same pair; every station block appears in some row. `row_index`: each visibility of an index of blk and a channel group appears in at most one row of that index and group; about half of the rows are -1.
All inputs are finite; a program needn't handle non-finite values. No bound on the sum of `flag_mask` on one device may be relied on, other than what follows from the above.
Results may differ from a plain program's by a relative error of at most 0.009.
Values may be sent and summed in bfloat16 or wider, within the bound.
A program may use at most 64 MiB of HBM per device.

v0:
```python
import math

import jax
import jax.numpy as jnp
from jax import lax
from jax.sharding import PartitionSpec as P

S = 512
BS = 32
ITERS = 3
TS = 128
KS = 8
OVER = 8


def kernel_rows(code_values):
    centre = code_values.astype(jnp.float32) / OVER
    cell_axis = jnp.arange(TS, dtype=jnp.float32)
    offset = cell_axis - centre[..., None]
    inside = jnp.abs(offset) < 0.5 * KS
    return jnp.where(inside, jnp.cos(math.pi * offset / KS) ** 2, 0.0).astype(jnp.bfloat16)


def grid_piece(real_rows, imag_rows, u_values, v_values):
    kernel_u = kernel_rows(u_values)
    kernel_v = kernel_rows(v_values).astype(jnp.float32)
    weighted = jnp.stack(
        (
            kernel_v * real_rows.astype(jnp.float32)[..., None],
            kernel_v * imag_rows.astype(jnp.float32)[..., None],
        ),
        axis=-2,
    ).astype(jnp.bfloat16)
    return jnp.einsum("grx,grcy->gcxy", kernel_u, weighted, preferred_element_type=jnp.float32)


def grid_groups(real_rows, imag_rows, u_values, v_values):
    tile_count = real_rows.shape[0]
    group_size = math.gcd(tile_count, 8)

    def regroup(member):
        return member.reshape((tile_count // group_size, group_size) + member.shape[1:])

    members = (regroup(real_rows), regroup(imag_rows), regroup(u_values), regroup(v_values))

    def advance(running, pieces):
        result = grid_piece(pieces[0], pieces[1], pieces[2], pieces[3])
        return (running + jnp.sum(result, axis=0), None)

    running, stacked = lax.scan(advance, jnp.zeros((2, TS, TS), jnp.float32), members)
    return running


def contract(form, left, right):
    return jnp.einsum(form, left, right, precision=lax.Precision.HIGHEST)


def block_gains(gain_real, gain_imag, onehot_first, onehot_second):
    tables = jnp.stack((gain_real, gain_imag)).reshape(2, S // BS, BS)
    return (
        contract("kn,cns->cks", onehot_first, tables),
        contract("kn,cns->cks", onehot_second, tables),
    )


def station_terms(
    cross_real, cross_imag, model_power, gain_real, gain_imag, onehot_first, onehot_second
):
    first_gains, second_gains = block_gains(gain_real, gain_imag, onehot_first, onehot_second)
    first_real, first_imag = (first_gains[0], first_gains[1])
    second_real, second_imag = (second_gains[0], second_gains[1])
    first_terms = jnp.stack(
        (
            contract("kij,kj->ki", cross_real, second_real)
            - contract("kij,kj->ki", cross_imag, second_imag),
            contract("kij,kj->ki", cross_real, second_imag)
            + contract("kij,kj->ki", cross_imag, second_real),
            contract(
                "kij,kj->ki", model_power, second_real * second_real + second_imag * second_imag
            ),
        )
    )
    second_terms = jnp.stack(
        (
            contract("kij,ki->kj", cross_real, first_real)
            + contract("kij,ki->kj", cross_imag, first_imag),
            contract("kij,ki->kj", cross_real, first_imag)
            - contract("kij,ki->kj", cross_imag, first_real),
            contract("kij,ki->kj", model_power, first_real * first_real + first_imag * first_imag),
        )
    )
    placed = contract("kn,cks->cns", onehot_first, first_terms) + contract(
        "kn,cks->cns", onehot_second, second_terms
    )
    placed = placed.reshape(3, S)
    return (placed[0], placed[1], placed[2])


def shards(
    pair_map, visibilities, model_vis, flag_mask, gain_amp, gain_phase, row_index, cell_codes
):
    moved_u, moved_v = (
        lax.all_to_all(cell_codes[0, 0, 0], "blk", split_axis=0, concat_axis=0, tiled=True),
        lax.all_to_all(cell_codes[1, 0, 0], "blk", split_axis=0, concat_axis=0, tiled=True),
    )
    slot_count = pair_map.shape[0]
    chan_count = visibilities.shape[2]
    block_count = S // BS
    baseline = jnp.arange(BS * BS, dtype=jnp.int32)
    first_block = pair_map[:, 0]
    second_block = pair_map[:, 1]
    first_station = first_block[:, None] * BS + baseline[None, :] // BS
    second_station = second_block[:, None] * BS + baseline[None, :] % BS
    weight = (
        flag_mask.astype(jnp.float32)
        * (first_station != second_station).astype(jnp.float32)[:, None, :]
    )
    weight = weight.reshape(slot_count, chan_count, BS, BS)
    square_shape = (slot_count, chan_count, BS, BS)
    vis_real = visibilities[0].astype(jnp.float32).reshape(square_shape)
    vis_imag = visibilities[1].astype(jnp.float32).reshape(square_shape)
    model_real = model_vis[0].astype(jnp.float32).reshape(square_shape)
    model_imag = model_vis[1].astype(jnp.float32).reshape(square_shape)
    cross_real = jnp.sum(weight * (vis_real * model_real + vis_imag * model_imag), axis=1)
    cross_imag = jnp.sum(weight * (vis_imag * model_real - vis_real * model_imag), axis=1)
    model_power = jnp.sum(weight * (model_real * model_real + model_imag * model_imag), axis=1)
    block_axis = jnp.arange(block_count, dtype=jnp.int32)
    onehot_first = (first_block[:, None] == block_axis[None, :]).astype(jnp.float32)
    onehot_second = (second_block[:, None] == block_axis[None, :]).astype(jnp.float32)
    gain_real = gain_amp * jnp.cos(gain_phase)
    gain_imag = gain_amp * jnp.sin(gain_phase)
    for sweep_index in range(ITERS):
        terms = station_terms(
            cross_real, cross_imag, model_power, gain_real, gain_imag, onehot_first, onehot_second
        )
        numerator_real, numerator_imag, denominator = lax.psum(
            (terms[0], terms[1], terms[2]), ("blk", "chan")
        )
        update_real = numerator_real / denominator
        update_imag = numerator_imag / denominator
        if sweep_index % 2 == 1:
            gain_real = 0.5 * (update_real + gain_real)
            gain_imag = 0.5 * (update_imag + gain_imag)
        else:
            gain_real = update_real
            gain_imag = update_imag
    first_gains, second_gains = block_gains(gain_real, gain_imag, onehot_first, onehot_second)
    first_real = first_gains[0][:, None, :, None]
    first_imag = first_gains[1][:, None, :, None]
    second_real = second_gains[0][:, None, None, :]
    second_imag = second_gains[1][:, None, None, :]
    twisted_real = model_real * second_real + model_imag * second_imag
    twisted_imag = model_imag * second_real - model_real * second_imag
    predicted_real = first_real * twisted_real - first_imag * twisted_imag
    predicted_imag = first_real * twisted_imag + first_imag * twisted_real
    resid_real = (weight * (vis_real - predicted_real)).astype(jnp.bfloat16).reshape(-1)
    resid_imag = (weight * (vis_imag - predicted_imag)).astype(jnp.bfloat16).reshape(-1)
    slot_rows = row_index[0, 0]
    live_rows = slot_rows >= 0
    safe_rows = jnp.where(live_rows, slot_rows, 0)
    rows_real = jnp.where(live_rows, resid_real[safe_rows], 0.0)
    rows_imag = jnp.where(live_rows, resid_imag[safe_rows], 0.0)
    got_real, got_imag = (
        lax.all_to_all(rows_real, "blk", split_axis=0, concat_axis=0, tiled=True),
        lax.all_to_all(rows_imag, "blk", split_axis=0, concat_axis=0, tiled=True),
    )
    owned = grid_groups(got_real, got_imag, moved_u, moved_v)[None]
    return (owned[None], jnp.stack((gain_real, gain_imag)))


def solution(mesh):
    in_specs = (
        P("blk", None),
        P(None, "blk", "chan", None),
        P(None, "blk", "chan", None),
        P("blk", "chan", None),
        P(),
        P(),
        P("chan", "blk", None, None),
        P(None, "chan", "blk", None, None),
    )
    out_specs = (P("chan", "blk", None, None, None), P())
    return jax.shard_map(shards, mesh=mesh, in_specs=in_specs, out_specs=out_specs, check_vma=False)
```

profile of v0, /device:TPU:0, one launch (start us, length us, event | category | flops | bytes accessed | tf_op | source)
XLA Modules:
  0.0 216.3 jit_solution(5365592436770304655)
XLA Ops:
  0.6 0.7 copy-done.4
  1.3 0.2 slice_reduce_fusion.1
  1.6 1.2 fusion.15
  2.9 0.6 copy-done.5
  3.7 0.2 convolution_bitcast_fusion.8
  4.2 0.2 fusion.115
  4.3 0.2 fusion.117
  4.5 0.2 fusion.114
  4.7 0.2 convolution_bitcast_fusion.7
  5.6 0.2 fusion.118
  5.8 0.2 fusion.123
  6.0 0.3 fusion.25
  6.2 0.3 fusion.2
  6.8 42.0 %all-reduce.2 = (f32[512]{0:T(512)S(1)}, f32[512]{0:T(512)S(1)}, f32[512]{0:T(512)S(1)}) all-reduce(f32[512]{0:T(512)S(1)} %squeeze.86, f32[512]{0:T(512)S(1)} %squeeze.87, f32[512]{0:T(512)S(1)} %squeeze.88), channel_id=1, replica_groups=mesh['blk'=8,'chan'=4] {'blk','chan'}, use_global_device_ids=true, to_apply=%region_3.4 | all-reduce | flops 1536 | bytes 12288 | tf_op jit(solution)/shard_map/psum | solution.py:136
  48.9 0.2 convolution_bitcast_fusion.5
  49.1 0.2 fusion.129
  49.8 0.2 convolution_bitcast_fusion.6
  50.0 0.2 fusion.124
  50.1 0.2 fusion.127
  50.3 0.2 fusion.125
  50.5 0.2 fusion.126
  50.6 0.2 fusion.133
  51.0 0.3 fusion.36
  51.3 0.3 fusion.1
  51.8 40.1 %all-reduce.1 = (f32[512]{0:T(512)S(1)}, f32[512]{0:T(512)S(1)}, f32[512]{0:T(512)S(1)}) all-reduce(f32[512]{0:T(512)S(1)} %squeeze.93, f32[512]{0:T(512)S(1)} %squeeze.94, f32[512]{0:T(512)S(1)} %squeeze.95), channel_id=1, replica_groups=mesh['blk'=8,'chan'=4] {'blk','chan'}, use_global_device_ids=true, to_apply=%region_6.7 | all-reduce | flops 1536 | bytes 12288 | tf_op jit(solution)/shard_map/psum | solution.py:136
  92.1 0.2 convolution_bitcast_fusion.3
  92.9 0.2 convolution_bitcast_fusion.4
  93.1 0.2 fusion.134
  93.3 0.2 fusion.137
  93.5 0.2 fusion.135
  93.6 0.2 fusion.136
  93.8 0.2 fusion.143
  94.2 0.3 fusion.47
  94.4 0.3 fusion
  95.0 39.9 %all-reduce = (f32[512]{0:T(512)S(1)}, f32[512]{0:T(512)S(1)}, f32[512]{0:T(512)S(1)}) all-reduce(f32[512]{0:T(512)S(1)} %squeeze.100, f32[512]{0:T(512)S(1)} %squeeze.101, f32[512]{0:T(512)S(1)} %squeeze.102), channel_id=1, replica_groups=mesh['blk'=8,'chan'=4] {'blk','chan'}, use_global_device_ids=true, to_apply=%region_9.10 | all-reduce | flops 1536 | bytes 12288 | tf_op jit(solution)/shard_map/psum | solution.py:136
  135.1 0.2 convolution_bitcast_fusion.1
  135.2 0.2 convolution_bitcast_fusion.2
  135.5 0.9 copy-done.1
  136.5 0.2 mul.274
  136.7 0.2 mul.278
  137.0 0.2 mul.271
  137.3 0.2 mul.283
  137.7 0.7 copy-done.2
  138.5 13.1 %gather_fusion.1 = bf16[2048]{0:T(1024)(128)(2,1)S(1)} fusion(bf16[32768]{0:T(1024)(128)(2,1)S(1)} %multiply_convert_fusion, s32[2048]{0:T(1024)S(1)} %broadcast_clamp_fusion), kind=kCustom, calls=%fused_computation.1 | custom fusion | bytes 16384 | tf_op jit(solution)/shard_map/gather | solution.py:162
  151.6 13.1 %gather_fusion = bf16[2048]{0:T(1024)(128)(2,1)S(1)} fusion(bf16[32768]{0:T(1024)(128)(2,1)S(1)} %get-tuple-element.46, s32[2048]{0:T(1024)S(1)} %broadcast_clamp_fusion), kind=kCustom, calls=%fused_computation | custom fusion | bytes 16384 | tf_op jit(solution)/shard_map/gather | solution.py:161
  164.7 0.5 broadcast.303
  165.2 0.6 reduce.13
  165.9 0.6 reshape.453
  166.5 5.4 %all-to-all-start.2 = ((bf16[8,2,128]{2,1,0:T(2,128)(2,1)}), bf16[8,2,128]{2,1,0:T(2,128)(2,1)S(1)}, u32[]{:S(2)}, u32[]{:S(2)}) async-start(bf16[8,2,128]{2,1,0:T(2,128)(2,1)} %reshape.453), calls=%async_computation.2 | async-start | bytes 8192 | tf_op jit(solution)/shard_map/all_to_all | solution.py:165
  171.9 0.6 reduce.12
  172.6 0.6 reshape.455
  173.2 5.2 %all-to-all-done.2 = bf16[8,2,128]{2,1,0:T(2,128)(2,1)S(1)} async-done(((bf16[8,2,128]{2,1,0:T(2,128)(2,1)}), bf16[8,2,128]{2,1,0:T(2,128)(2,1)S(1)}, u32[]{:S(2)}, u32[]{:S(2)}) %all-to-all-start.2) | async-done | bytes 4128 | tf_op jit(solution)/shard_map/all_to_all | solution.py:165
  178.3 3.3 %all-to-all-start.1 = ((bf16[8,2,128]{2,1,0:T(2,128)(2,1)}), bf16[8,2,128]{2,1,0:T(2,128)(2,1)S(1)}, u32[]{:S(2)}, u32[]{:S(2)}) async-start(bf16[8,2,128]{2,1,0:T(2,128)(2,1)} %reshape.455), calls=%async_computation.1 | async-start | bytes 8192 | tf_op jit(solution)/shard_map/all_to_all | solution.py:164
  181.7 0.6 copy.88
  182.3 5.7 %all-to-all-done.1 = bf16[8,2,128]{2,1,0:T(2,128)(2,1)S(1)} async-done(((bf16[8,2,128]{2,1,0:T(2,128)(2,1)}), bf16[8,2,128]{2,1,0:T(2,128)(2,1)S(1)}, u32[]{:S(2)}, u32[]{:S(2)}) %all-to-all-start.1) | async-done | bytes 4128 | tf_op jit(solution)/shard_map/all_to_all | solution.py:164
  188.0 3.3 %all-to-all-start = ((s32[8,1,256]{2,1,0:T(1,128)}), s32[8,1,256]{2,1,0:T(1,128)S(1)}, u32[]{:S(2)}, u32[]{:S(2)}) async-start(s32[8,1,256]{2,1,0:T(1,128)} %bitcast.384), calls=%async_computation | async-start | bytes 16384 | tf_op jit(solution)/shard_map/all_to_all | solution.py:104
  191.3 0.6 pad_maximum_fusion
  191.9 0.6 copy.87
  192.6 5.2 %all-to-all-done = s32[8,1,256]{2,1,0:T(1,128)S(1)} async-done(((s32[8,1,256]{2,1,0:T(1,128)}), s32[8,1,256]{2,1,0:T(1,128)S(1)}, u32[]{:S(2)}, u32[]{:S(2)}) %all-to-all-start) | async-done | bytes 8224 | tf_op jit(solution)/shard_map/all_to_all | solution.py:104
  197.8 3.5 %all-to-all-start.3 = ((s32[8,1,256]{2,1,0:T(1,128)}), s32[8,1,256]{2,1,0:T(1,128)S(1)}, u32[]{:S(2)}, u32[]{:S(2)}) async-start(s32[8,1,256]{2,1,0:T(1,128)} %bitcast.383), calls=%async_computation.3 | async-start | bytes 16384 | tf_op jit(solution)/shard_map/all_to_all | solution.py:103
  201.3 6.2 %all-to-all-done.3 = s32[8,1,256]{2,1,0:T(1,128)S(1)} async-done(((s32[8,1,256]{2,1,0:T(1,128)}), s32[8,1,256]{2,1,0:T(1,128)S(1)}, u32[]{:S(2)}, u32[]{:S(2)}) %all-to-all-start.3) | async-done | bytes 8224 | tf_op jit(solution)/shard_map/all_to_all | solution.py:103
  207.6 3.8 %fusion.3 = (bf16[8,256,1,128]{1,3,0,2:T(8,128)(2,1)S(1)}, bf16[8,256,1,128]{1,3,0,2:T(8,128)(2,1)S(1)}) fusion(f32[8,256]{1,0:T(8,128)S(1)} %bitcast.401, f32[8,256]{1,0:T(8,128)S(1)} %bitcast.402, f32[8,256]{1,0:T(8,128)S(1)} %bitcast.400), kind=kLoop, calls=%fused_computation.19 | loop fusion | flops 3145728 | bytes 1073152 | tf_op jit(solution)/shard_map/convert.6
  211.4 4.1 %convolution_bitcast_fusion = f32[1,1,2,128,128]{3,4,2,1,0:T(8,128)S(1)} fusion(bf16[8,256,1,128]{1,3,0,2:T(8,128)(2,1)S(1)} %get-tuple-element.66, bf16[8,256,1,128]{1,3,0,2:T(8,128)(2,1)S(1)} %get-tuple-element.65, f32[8,256]{1,0:T(8,128)S(1)} %bitcast.430), kind=kOutput, calls=%fused_computation.4 | convolution fusion | flops 136577024 | bytes 1187840 | tf_op jit(solution)/shard_map/while/body/eval_jaxpr/grx,grcy->gcxy/dot_general | solution.py:34
  215.5 0.8 copy.19
  (116 shorter events, 4.8 us)
Async XLA Ops:
  0.6 0.7 copy-start.4
  2.8 0.7 copy-start.5
  2.8 0.7 copy-start.6
  94.7 40.7 %copy-start = (bf16[2,2,16,1024]{3,2,1,0:T(8,128)(2,1)S(1)}, bf16[2,2,16,1024]{3,2,1,0:T(8,128)(2,1)}, u32[]{:S(2)}) copy-start(bf16[2,2,16,1024]{3,2,1,0:T(8,128)(2,1)} %param.9) | copy-start | bytes 393220
  135.4 0.9 copy-start.1
  137.6 0.7 copy-start.2
  166.5 15.2 %copy-start.3 = (s32[2,1,1,8,256]{4,3,2,1,0:T(8,128)S(1)}, s32[2,1,1,8,256]{4,3,2,1,0:T(8,128)}, u32[]{:S(2)}) copy-start(s32[2,1,1,8,256]{4,3,2,1,0:T(8,128)} %param.15) | copy-start | bytes 49156
  166.5 11.9 %all-to-all-start.2 = ((bf16[8,2,128]{2,1,0:T(2,128)(2,1)}), bf16[8,2,128]{2,1,0:T(2,128)(2,1)S(1)}, u32[]{:S(2)}, u32[]{:S(2)}) async-start(bf16[8,2,128]{2,1,0:T(2,128)(2,1)} %reshape.453), calls=%async_computation.2 | async-start | bytes 8192 | tf_op jit(solution)/shard_map/all_to_all | solution.py:165
  178.3 9.7 %all-to-all-start.1 = ((bf16[8,2,128]{2,1,0:T(2,128)(2,1)}), bf16[8,2,128]{2,1,0:T(2,128)(2,1)S(1)}, u32[]{:S(2)}, u32[]{:S(2)}) async-start(bf16[8,2,128]{2,1,0:T(2,128)(2,1)} %reshape.455), calls=%async_computation.1 | async-start | bytes 8192 | tf_op jit(solution)/shard_map/all_to_all | solution.py:164
  188.0 9.8 %all-to-all-start = ((s32[8,1,256]{2,1,0:T(1,128)}), s32[8,1,256]{2,1,0:T(1,128)S(1)}, u32[]{:S(2)}, u32[]{:S(2)}) async-start(s32[8,1,256]{2,1,0:T(1,128)} %bitcast.384), calls=%async_computation | async-start | bytes 16384 | tf_op jit(solution)/shard_map/all_to_all | solution.py:104
  197.8 9.8 %all-to-all-start.3 = ((s32[8,1,256]{2,1,0:T(1,128)}), s32[8,1,256]{2,1,0:T(1,128)S(1)}, u32[]{:S(2)}, u32[]{:S(2)}) async-start(s32[8,1,256]{2,1,0:T(1,128)} %bitcast.383), calls=%async_computation.3 | async-start | bytes 16384 | tf_op jit(solution)/shard_map/all_to_all | solution.py:103
where the time goes:
time: 217 us; the launch traced here: 216 us
  blocking collectives  122 us (56%)
  local copies, waits for them, and re-layouts  35.5 us (16%)
  waiting for transfers between devices  22.3 us (10%)
  starting transfers between devices  15.6 us (7%)
  matrix products  12.1 us (6%)
  other arithmetic  7.54 us (3%)
    psum x3, blocking collectives, shards(): lax.psum((terms[0], terms[1], terms[2]), ('blk', 'chan'))  122 us
    gather x2, local copies, waits for them, and re-layouts, shards(): rows_imag = jnp.where(live_rows, resid_imag[safe_rows], 0.0)  13.1 us
    gather x2, local copies, waits for them, and re-layouts, shards(): rows_real = jnp.where(live_rows, resid_real[safe_rows], 0.0)  13.1 us
    dot_general x44, matrix products, contract(): return jnp.einsum(form, left, right, precision=lax.Precision.HIGHEST)  8.03 us
    all_to_all x1, waiting for transfers between devices, shards(): lax.all_to_all(cell_codes[0, 0, 0], 'blk', split_axis=0, concat_axis=0, t...  6.25 us
    unnamed x35, local copies, waits for them, and re-layouts  6.19 us
    all_to_all x1, waiting for transfers between devices, shards(): lax.all_to_all(rows_real, 'blk', split_axis=0, concat_axis=0, tiled=True)  5.72 us
    all_to_all x1, starting transfers between devices, shards(): lax.all_to_all(rows_imag, 'blk', split_axis=0, concat_axis=0, tiled=True)  5.44 us
  transfers between devices with their start and end apart: 4, of which 4 were waited for; matrix products, arithmetic and copies ran while one was open for 1% of the time, Pallas kernels for 0%

commit v1 on v0

v1 whole, which is shorter than its diff:
```python
import functools
import math

import jax
import jax.numpy as jnp
from jax import lax
from jax.experimental import pallas as pl
from jax.experimental.pallas import tpu as pltpu
from jax.sharding import PartitionSpec as P

ITERS = 3
TS = 128
KS = 8
OVER = 8
LANES = 128
MESH = pl.DeviceIdType.MESH
F32 = jnp.float32
BF16 = jnp.bfloat16


def iota(shape, dim):
    return lax.broadcasted_iota(jnp.int32, shape, dim)


def split3(x):
    hi = x.astype(BF16)
    rest = x - hi.astype(F32)
    mid = rest.astype(BF16)
    low = (rest - mid.astype(F32)).astype(BF16)
    return hi, mid, low


def dot(a, b):
    return jnp.dot(a, b, preferred_element_type=F32)


def loop(count, body, carry):
    if count <= 8:
        for step in range(count):
            carry = body(step, carry)
        return carry
    return lax.fori_loop(0, count, body, carry)


def kernel(
    n_blk,
    n_chan,
    pm_ref,
    vis_ref,
    mod_ref,
    flag_ref,
    amp_ref,
    ph_ref,
    ri_ref,
    cc_ref,
    grid_ref,
    gains_ref,
    rs_src,
    rs_dst,
    ag_src,
    ag_buf,
    data_t,
    row_src,
    row_buf,
    ku_buf,
    kv_buf,
    pa_buf,
    pb_buf,
    ex_a,
    ex_b,
    fold_ab,
    rs_send,
    rs_recv,
    ag_send,
    ag_recv,
    row_send,
    row_recv,
):
    blk = lax.axis_index("blk")
    chan = lax.axis_index("chan")
    n_dev = n_blk * n_chan
    me = blk * n_chan + chan
    slots, n_ch, n_base = vis_ref.shape[1:]
    stations = amp_ref.shape[1]
    side = math.isqrt(n_base)
    quads = stations // LANES
    per = LANES // side
    cuts = n_base // LANES
    halves = cuts // n_chan
    piece = halves * 8
    rows = row_buf.shape[2]
    pairs = slots * n_blk

    def device(step):
        target = lax.rem(me + step, n_dev)
        return (target // n_chan, lax.rem(target, n_chan))

    barrier = pltpu.get_barrier_semaphore()

    def greet(step, carry):
        pl.semaphore_signal(barrier, inc=1, device_id=device(step), device_id_type=MESH)
        return carry

    lax.fori_loop(1, n_dev, greet, 0)

    base = iota((1, n_base), 1)
    same_place = (base // side) == (base % side)
    pm = pm_ref[...]
    sums = []
    masked = [[], [], [], []]
    for slot in range(slots):
        same_block = pm[slot : slot + 1, 0:1] == pm[slot : slot + 1, 1:2]
        keep = jnp.where(jnp.logical_and(same_place, same_block), 0.0, 1.0)
        weight = flag_ref[slot].astype(F32) * keep
        vr = vis_ref[0, slot].astype(F32) * weight
        vi = vis_ref[1, slot].astype(F32) * weight
        mr = mod_ref[0, slot].astype(F32) * weight
        mi = mod_ref[1, slot].astype(F32) * weight
        for held, value in zip(masked, (vr, vi, mr, mi)):
            held.append(value)
        sums.append(
            (
                jnp.sum(vr * mr + vi * mi, axis=0, keepdims=True),
                jnp.sum(vi * mr - vr * mi, axis=0, keepdims=True),
                jnp.sum(mr * mr + mi * mi, axis=0, keepdims=True),
            )
        )
    level = iota((8, n_base), 0)
    stacked = jnp.zeros((8, n_base), F32)
    for comp in range(3):
        for slot in range(slots):
            stacked = jnp.where(level == comp * slots + slot, sums[slot][comp], stacked)
    for c in range(n_chan):
        for half in range(halves):
            cut = (c * halves + half) * LANES
            rs_src[c, half * 8 : half * 8 + 8, :] = stacked[:, cut : cut + LANES]
    tile_rows = slots * n_ch
    for part in range(4):
        full = jnp.concatenate(masked[part], axis=0)
        tall = jnp.concatenate(
            [full[:, cut * LANES : (cut + 1) * LANES] for cut in range(cuts)], axis=0
        )
        data_t[part * LANES : (part + 1) * LANES, :] = tall.T.astype(BF16)

    pl.semaphore_wait(barrier, n_dev - 1)

    rs_copies = []
    for step in range(1, n_chan):
        other = lax.rem(chan + step, n_chan)
        copy = pltpu.make_async_remote_copy(
            src_ref=rs_src.at[other],
            dst_ref=rs_dst.at[step],
            send_sem=rs_send.at[step],
            recv_sem=rs_recv.at[step],
            device_id=(blk, other),
            device_id_type=MESH,
        )
        copy.start()
        rs_copies.append(copy)

    hi_axis = iota((tile_rows * cuts, rows), 0)
    lo_axis = iota((LANES, rows), 0)

    def row_copy(step):
        tile = lax.rem(blk + step, n_blk)
        return pltpu.make_async_remote_copy(
            src_ref=row_src.at[tile],
            dst_ref=row_buf.at[blk],
            send_sem=row_send.at[step],
            recv_sem=row_recv.at[step],
            device_id=(tile, chan),
            device_id_type=MESH,
        )

    def make_rows(tile, out_ref, where):
        place = ri_ref[0, 0, pl.ds(tile, 1), :]
        high = ((place // LANES) % cuts) * tile_rows + place // n_base
        high = jnp.where(place < 0, -1, high)
        low = jnp.where(place < 0, 0, place) % LANES
        pick = jnp.where(hi_axis == high, 1.0, 0.0).astype(BF16)
        got = dot(data_t[...], pick)
        out_ref[where, 0:1, :] = cc_ref[0, 0, 0, pl.ds(tile, 1), :].astype(F32)
        out_ref[where, 1:2, :] = cc_ref[1, 0, 0, pl.ds(tile, 1), :].astype(F32)
        out_ref[where, 2:3, :] = place.astype(F32)
        for part in range(4):
            block = got[part * LANES : (part + 1) * LANES]
            out_ref[where, 3 + part : 4 + part, :] = jnp.sum(
                jnp.where(lo_axis == low, block, 0.0), axis=0, keepdims=True
            )
        out_ref[where, 7:8, :] = jnp.zeros((1, rows), F32)

    def send_rows(step, carry):
        make_rows(lax.rem(blk + step + 1, n_blk), row_src, lax.rem(blk + step + 1, n_blk))
        row_copy(step + 1).start()
        return carry

    loop(n_blk - 1, send_rows, 0)

    for copy in rs_copies:
        copy.wait_recv()
    total = rs_src[chan]
    for step in range(1, n_chan):
        total = total + rs_dst[step]
    sub = iota((piece, LANES), 0)
    for slot in range(slots):
        for which in range(2):
            value = pm[slot : slot + 1, which : which + 1].astype(F32)
            total = jnp.where(sub == slot * 8 + 6 + which, value, total)
    ag_src[...] = total
    own = pl.multiple_of((chan * n_blk + blk) * piece, 8)
    ag_buf[pl.ds(own, piece), :] = total

    def ag_copy(step):
        return pltpu.make_async_remote_copy(
            src_ref=ag_src,
            dst_ref=ag_buf.at[pl.ds(own, piece), :],
            send_sem=ag_send.at[step],
            recv_sem=ag_recv.at[step],
            device_id=device(step),
            device_id_type=MESH,
        )

    def ag_start(step, carry):
        ag_copy(step).start()
        return carry

    lax.fori_loop(1, n_dev, ag_start, 0)

    make_rows(blk, row_buf, blk)

    el = iota((LANES, n_base), 0) % side
    et = iota((LANES, n_base), 1)
    ex_a[...] = jnp.where(el == et // side, 1.0, 0.0).astype(BF16)
    ex_b[...] = jnp.where(el == et % side, 1.0, 0.0).astype(BF16)
    ft = iota((n_base, LANES), 0)
    fl = iota((n_base, LANES), 1) % side
    fold_ab[:, :LANES] = jnp.where(fl == ft // side, 1.0, 0.0).astype(BF16)
    fold_ab[:, LANES:] = jnp.where(fl == ft % side, 1.0, 0.0).astype(BF16)
    amp = amp_ref[...]
    phase = ph_ref[...]
    gain_real = amp * jnp.cos(phase)
    gain_imag = amp * jnp.sin(phase)

    def row_wait(step, carry):
        row_copy(step + 1).wait_recv()
        return carry

    loop(n_blk - 1, row_wait, 0)

    cell = iota((TS, LANES), 0)
    turn = (cell % (2 * KS)).astype(F32) * (math.pi / KS)
    cell_cos = jnp.cos(turn)[:, 0:1]
    cell_sin = jnp.sin(turn)[:, 0:1]
    cell_at = cell[:, 0:1].astype(F32) * OVER
    lane_side = iota((LANES, rows), 0) % side

    def taper(code):
        code_i = code.astype(jnp.int32)
        angle = (code_i % (2 * KS * OVER)).astype(F32) * (math.pi / (KS * OVER))
        wave = cell_cos * jnp.cos(angle) + cell_sin * jnp.sin(angle)
        inside = jnp.abs(cell_at - code) < 0.5 * KS * OVER
        return jnp.where(inside, wave * wave, 0.0).astype(BF16)

    def prepare(k, carry):
        ku_buf[k] = taper(row_buf[k, 0:1, :])
        kv_buf[k] = taper(row_buf[k, 1:2, :])
        place = row_buf[k, 2:3, :].astype(jnp.int32)
        place = jnp.where(place < 0, 0, place)
        pa_buf[k] = jnp.where(lane_side == (place // side) % side, 1.0, 0.0).astype(BF16)
        pb_buf[k] = jnp.where(lane_side == place % side, 1.0, 0.0).astype(BF16)
        return carry

    loop(n_blk, prepare, 0)

    def ag_wait(step, carry):
        ag_copy(step).wait_recv()
        return carry

    lax.fori_loop(1, n_dev, ag_wait, 0)

    def gathered(c, half, row):
        start = c * n_blk * piece + half * 8 + row
        return ag_buf[pl.ds(start, n_blk, stride=piece), :]

    def whole(comp):
        return jnp.concatenate(
            [
                jnp.concatenate(
                    [
                        gathered(c, half, comp * slots + slot)
                        for c in range(n_chan)
                        for half in range(halves)
                    ],
                    axis=1,
                )
                for slot in range(slots)
            ],
            axis=0,
        )

    cross_real, cross_imag, power = whole(0), whole(1), whole(2)
    first = jnp.concatenate([gathered(0, slot, 6) for slot in range(slots)], axis=0)
    second = jnp.concatenate([gathered(0, slot, 7) for slot in range(slots)], axis=0)
    lane_block = iota((pairs, LANES), 1) // side
    mask_a = [first.astype(jnp.int32) == lane_block + per * q for q in range(quads)]
    mask_b = [second.astype(jnp.int32) == lane_block + per * q for q in range(quads)]

    def chosen(gain, mask):
        out = jnp.zeros((pairs, LANES), F32)
        for q in range(quads):
            out = out + jnp.where(mask[q], gain[:, q * LANES : (q + 1) * LANES], 0.0)
        return out

    def pieces(real, imag, mask):
        return jnp.concatenate(split3(chosen(real, mask)) + split3(chosen(imag, mask)), axis=0)

    def joined(x):
        parts = [x[i * pairs : (i + 1) * pairs] for i in range(6)]
        return parts[0] + parts[1] + parts[2], parts[3] + parts[4] + parts[5]

    def placed(first_term, second_term):
        cols = []
        for q in range(quads):
            cols.append(
                jnp.sum(
                    jnp.where(mask_a[q], first_term, 0.0) + jnp.where(mask_b[q], second_term, 0.0),
                    axis=0,
                    keepdims=True,
                )
            )
        return jnp.concatenate(cols, axis=1)

    for sweep in range(ITERS):
        fr, fi = joined(dot(pieces(gain_real, gain_imag, mask_a), ex_a[...]))
        sr, si = joined(dot(pieces(gain_real, gain_imag, mask_b), ex_b[...]))
        terms = jnp.concatenate(
            (
                cross_real * sr - cross_imag * si,
                cross_real * si + cross_imag * sr,
                power * (sr * sr + si * si),
                cross_real * fr + cross_imag * fi,
                cross_real * fi - cross_imag * fr,
                power * (fr * fr + fi * fi),
            ),
            axis=0,
        )
        hi, mid, low = split3(terms)
        folded = dot(hi, fold_ab[...]) + dot(mid, fold_ab[...]) + dot(low, fold_ab[...])
        num_real, num_imag, den = (
            placed(
                folded[c * pairs : (c + 1) * pairs, :LANES],
                folded[(3 + c) * pairs : (4 + c) * pairs, LANES:],
            )
            for c in range(3)
        )
        update_real = num_real / den
        update_imag = num_imag / den
        if sweep % 2 == 1:
            gain_real = 0.5 * (update_real + gain_real)
            gain_imag = 0.5 * (update_imag + gain_imag)
        else:
            gain_real = update_real
            gain_imag = update_imag

    gains_ref[0:1, :] = gain_real
    gains_ref[1:2, :] = gain_imag

    table_a = pieces(gain_real, gain_imag, mask_a)
    table_b = pieces(gain_real, gain_imag, mask_b)
    pair_axis = iota((pairs, rows), 0)

    def grid_rows(k, acc):
        place = row_buf[k, 2:3, :].astype(jnp.int32)
        pair = (jnp.where(place < 0, 0, place) // (n_ch * n_base)) * n_blk + k
        hit = pair_axis == pair

        def pick(x):
            return jnp.sum(jnp.where(hit, x, 0.0), axis=0, keepdims=True)

        ar, ai = (pick(x) for x in joined(dot(table_a, pa_buf[k])))
        br, bi = (pick(x) for x in joined(dot(table_b, pb_buf[k])))
        vr, vi = row_buf[k, 3:4, :], row_buf[k, 4:5, :]
        mr, mi = row_buf[k, 5:6, :], row_buf[k, 6:7, :]
        tr = mr * br + mi * bi
        ti = mi * br - mr * bi
        live = place >= 0
        rr = jnp.where(live, vr - (ar * tr - ai * ti), 0.0).astype(BF16).astype(F32)
        ri = jnp.where(live, vi - (ar * ti + ai * tr), 0.0).astype(BF16).astype(F32)
        kv = kv_buf[k].astype(F32)
        h = jnp.concatenate(((kv * rr).astype(BF16), (kv * ri).astype(BF16)), axis=0)
        return acc + lax.dot_general(
            ku_buf[k], h, (((1,), (1,)), ((), ())), preferred_element_type=F32
        )

    acc = loop(n_blk, grid_rows, jnp.zeros((TS, 2 * TS), F32))
    grid_ref[0, 0, 0] = acc[:, :TS]
    grid_ref[0, 0, 1] = acc[:, TS:]

    for copy in rs_copies:
        copy.wait_send()

    def ag_done(step, carry):
        ag_copy(step).wait_send()
        return carry

    lax.fori_loop(1, n_dev, ag_done, 0)

    def row_done(step, carry):
        row_copy(step + 1).wait_send()
        return carry

    loop(n_blk - 1, row_done, 0)


def shards(
    n_blk, n_chan, pair_map, visibilities, model_vis, flag_mask, gain_amp, gain_phase, row_index, cell_codes
):
    slots, n_ch, n_base = visibilities.shape[1:]
    stations = gain_amp.shape[0]
    rows = row_index.shape[-1]
    n_dev = n_blk * n_chan
    piece = n_base // LANES // n_chan * 8
    dma = pltpu.SemaphoreType.DMA
    return pl.pallas_call(
        functools.partial(kernel, n_blk, n_chan),
        out_shape=(
            jax.ShapeDtypeStruct((1, 1, 2, TS, TS), F32),
            jax.ShapeDtypeStruct((2, stations), F32),
        ),
        in_specs=[pl.BlockSpec(memory_space=pltpu.VMEM)] * 8,
        out_specs=(pl.BlockSpec(memory_space=pltpu.VMEM),) * 2,
        scratch_shapes=[
            pltpu.VMEM((n_chan, piece, LANES), F32),
            pltpu.VMEM((n_chan, piece, LANES), F32),
            pltpu.VMEM((piece, LANES), F32),
            pltpu.VMEM((n_dev * piece, LANES), F32),
            pltpu.VMEM((4 * LANES, slots * n_ch * n_base // LANES), BF16),
            pltpu.VMEM((n_blk, 8, rows), F32),
            pltpu.VMEM((n_blk, 8, rows), F32),
            pltpu.VMEM((n_blk, TS, rows), BF16),
            pltpu.VMEM((n_blk, TS, rows), BF16),
            pltpu.VMEM((n_blk, LANES, rows), BF16),
            pltpu.VMEM((n_blk, LANES, rows), BF16),
            pltpu.VMEM((LANES, n_base), BF16),
            pltpu.VMEM((LANES, n_base), BF16),
            pltpu.VMEM((n_base, 2 * LANES), BF16),
            dma((n_chan,)),
            dma((n_chan,)),
            dma((n_dev,)),
            dma((n_dev,)),
            dma((n_blk,)),
            dma((n_blk,)),
        ],
        compiler_params=pltpu.CompilerParams(
            collective_id=0, has_side_effects=True, vmem_limit_bytes=56 * 1024 * 1024
        ),
        name="solve_and_grid",
    )(
        pair_map,
        visibilities,
        model_vis,
        flag_mask,
        gain_amp.reshape(1, stations),
        gain_phase.reshape(1, stations),
        row_index,
        cell_codes,
    )


def solution(mesh):
    n_blk, n_chan = mesh.shape["blk"], mesh.shape["chan"]
    in_specs = (
        P("blk", None),
        P(None, "blk", "chan", None),
        P(None, "blk", "chan", None),
        P("blk", "chan", None),
        P(),
        P(),
        P("chan", "blk", None, None),
        P(None, "chan", "blk", None, None),
    )
    out_specs = (P("chan", "blk", None, None, None), P())
    return jax.shard_map(
        functools.partial(shards, n_blk, n_chan),
        mesh=mesh,
        in_specs=in_specs,
        out_specs=out_specs,
        check_vma=False,
    )
```

time: 217 us -> 24.7 us (0.11)
  blocking collectives: 122 us -> 0 us
  local copies, waits for them, and re-layouts: 35.5 us -> 2.17 us
  waiting for transfers between devices: 22.3 us -> 0 us
  Pallas kernels: 0 us -> 21.6 us
  starting transfers between devices: 15.6 us -> 0 us
  matrix products: 12.1 us -> 0 us
  other arithmetic: 7.54 us -> 0 us
    psum x3 -> x0, blocking collectives: 122 us -> none  [shards(): lax.psum((terms[0], terms[1], terms[2]), ('blk', 'chan'))]
    gather x4 -> x0, local copies, waits for them, and re-layouts: 26.2 us -> none  [the longest x2 13.1 us: shards(): rows_imag = jnp.where(live_rows, resid_imag[safe_rows], 0.0)]
    all_to_all x4 -> x0, waiting for transfers between devices: 22.3 us -> none  [the longest x1 6.25 us: shards(): lax.all_to_all(cell_codes[0, 0, 0], 'blk', split_axis=0, concat_axis=0, t...]
    pallas_call x0 -> x1, Pallas kernels: none -> 21.6 us  [shards(): pl.pallas_call(functools.partial(kernel, n_blk, n_chan), out_shape=(jax.S...]
    all_to_all x4 -> x0, starting transfers between devices: 15.6 us -> none  [the longest x1 5.44 us: shards(): lax.all_to_all(rows_imag, 'blk', split_axis=0, concat_axis=0, tiled=True)]
    dot_general x45 -> x0, matrix products: 12.1 us -> none  [the longest x44 8.03 us: contract(): return jnp.einsum(form, left, right, precision=lax.Precision.HIGHEST)]
    another operation x14 -> x0, other arithmetic: 4.48 us -> none
    unnamed x35 -> x4, local copies, waits for them, and re-layouts: 6.19 us -> 2.17 us
  transfers between devices with their start and end apart: 4 -> 0, of which waited for: 4 -> 0; matrix products, arithmetic and copies ran while one was open for 1% -> 0% of each run, Pallas kernels for 0% -> 0%
where the time goes in v1:
time: 24.7 us; the launch traced here: 24.4 us
  Pallas kernels  21.6 us (87%)
  local copies, waits for them, and re-layouts  2.17 us (9%)
  between operations  0.65 us (3%)
    pallas_call x1, Pallas kernels, shards(): pl.pallas_call(functools.partial(kernel, n_blk, n_chan), out_shape=(jax.S...  21.6 us
    unnamed x4, local copies, waits for them, and re-layouts  2.17 us

profile of v1, /device:TPU:0, one launch (start us, length us, event | category | flops | bytes accessed | tf_op | source)
XLA Modules:
  0.0 24.4 jit_solution(2007972606176977512)
XLA Ops:
  0.6 21.6 %solve_and_grid.1 = (f32[1,1,2,128,128]{4,3,2,1,0:T(8,128)}, f32[2,512]{1,0:T(2,128)}) custom-call(s32[2,2]{1,0:T(2,128)} %pm_ref.1, bf16[2,2,16,1024]{3,2,1,0:T(8,128)(2,1)} %vis_ref.1, bf16[2,2,16,1024]{3,2,1,0:T(8,128)(2,1)} %mod_ref.1, s32[2,16,1024]{2,1,0:T(8,128)} %flag_ref.1, f32[1,512]{1,0:T(1,128)} %bitcast.2, f32[1,512]{1,0:T(1,128)} %bitcast.3, ...), custom_call_target="tpu_custom_call" | custom-call | tf_op jit(solution)/shard_map/solve_and_grid/pallas_call | solution.py:424
  22.3 0.0 copy-start
  22.3 1.6 %copy.12 = f32[1,1,2,128,128]{4,3,2,1,0:T(8,128)} copy(f32[1,1,2,128,128]{4,3,2,1,0:T(8,128)} %get-tuple-element.4) | data formatting | bytes 262144
  23.9 0.0 copy-done
  23.9 0.6 %copy.13 = f32[2,512]{1,0:T(2,128)} copy(f32[2,512]{1,0:T(2,128)S(1)} %copy-done) | data formatting | bytes 8192
Async XLA Ops:
  22.3 1.6 %copy-start = (f32[2,512]{1,0:T(2,128)S(1)}, f32[2,512]{1,0:T(2,128)}, u32[]{:S(2)}) copy-start(f32[2,512]{1,0:T(2,128)} %get-tuple-element.5) | copy-start | bytes 12292

commit v2 on v1

--- a/solution.py
+++ b/solution.py
@@ -45,6 +45,16 @@
 def kernel(
     n_blk,
     n_chan,
+    pm_hbm,
+    vis_hbm,
+    mod_hbm,
+    flag_hbm,
+    amp_hbm,
+    ph_hbm,
+    ri_hbm,
+    cc_hbm,
+    grid_ref,
+    gains_ref,
     pm_ref,
     vis_ref,
     mod_ref,
@@ -53,13 +63,13 @@
     ph_ref,
     ri_ref,
     cc_ref,
-    grid_ref,
-    gains_ref,
     rs_src,
     rs_dst,
     ag_src,
     ag_buf,
     data_t,
+    code_src,
+    code_buf,
     row_src,
     row_buf,
     ku_buf,
@@ -73,8 +83,11 @@
     rs_recv,
     ag_send,
     ag_recv,
+    code_send,
+    code_recv,
     row_send,
     row_recv,
+    in_sem,
 ):
     blk = lax.axis_index("blk")
     chan = lax.axis_index("chan")
@@ -95,6 +108,23 @@
         target = lax.rem(me + step, n_dev)
         return (target // n_chan, lax.rem(target, n_chan))
 
+    loads = [
+        pltpu.make_async_copy(src, dst, in_sem.at[i])
+        for i, (src, dst) in enumerate(
+            (
+                (vis_hbm, vis_ref),
+                (mod_hbm, mod_ref),
+                (flag_hbm, flag_ref),
+                (pm_hbm, pm_ref),
+                (ri_hbm, ri_ref),
+                (cc_hbm, cc_ref),
+                (amp_hbm, amp_ref),
+                (ph_hbm, ph_ref),
+            )
+        )
+    ]
+    for load in loads:
+        load.start()
     barrier = pltpu.get_barrier_semaphore()
 
     def greet(step, carry):
@@ -102,6 +132,9 @@
         return carry
 
     lax.fori_loop(1, n_dev, greet, 0)
+
+    for load in loads[:4]:
+        load.wait()
 
     base = iota((1, n_base), 1)
     same_place = (base // side) == (base % side)
@@ -134,14 +167,6 @@
         for half in range(halves):
             cut = (c * halves + half) * LANES
             rs_src[c, half * 8 : half * 8 + 8, :] = stacked[:, cut : cut + LANES]
-    tile_rows = slots * n_ch
-    for part in range(4):
-        full = jnp.concatenate(masked[part], axis=0)
-        tall = jnp.concatenate(
-            [full[:, cut * LANES : (cut + 1) * LANES] for cut in range(cuts)], axis=0
-        )
-        data_t[part * LANES : (part + 1) * LANES, :] = tall.T.astype(BF16)
-
     pl.semaphore_wait(barrier, n_dev - 1)
 
     rs_copies = []
@@ -158,43 +183,45 @@
         copy.start()
         rs_copies.append(copy)
 
-    hi_axis = iota((tile_rows * cuts, rows), 0)
-    lo_axis = iota((LANES, rows), 0)
-
-    def row_copy(step):
+    for load in loads[4:]:
+        load.wait()
+
+    def hand_over(src, dst, send, recv, step):
         tile = lax.rem(blk + step, n_blk)
         return pltpu.make_async_remote_copy(
-            src_ref=row_src.at[tile],
-            dst_ref=row_buf.at[blk],
-            send_sem=row_send.at[step],
-            recv_sem=row_recv.at[step],
+            src_ref=src.at[tile],
+            dst_ref=dst.at[blk],
+            send_sem=send.at[step],
+            recv_sem=recv.at[step],
             device_id=(tile, chan),
             device_id_type=MESH,
         )
 
-    def make_rows(tile, out_ref, where):
-        place = ri_ref[0, 0, pl.ds(tile, 1), :]
-        high = ((place // LANES) % cuts) * tile_rows + place // n_base
-        high = jnp.where(place < 0, -1, high)
-        low = jnp.where(place < 0, 0, place) % LANES
-        pick = jnp.where(hi_axis == high, 1.0, 0.0).astype(BF16)
-        got = dot(data_t[...], pick)
+    code_copy = functools.partial(hand_over, code_src, code_buf, code_send, code_recv)
+    row_copy = functools.partial(hand_over, row_src, row_buf, row_send, row_recv)
+
+    def make_codes(tile, out_ref, where):
         out_ref[where, 0:1, :] = cc_ref[0, 0, 0, pl.ds(tile, 1), :].astype(F32)
         out_ref[where, 1:2, :] = cc_ref[1, 0, 0, pl.ds(tile, 1), :].astype(F32)
-        out_ref[where, 2:3, :] = place.astype(F32)
-        for part in range(4):
-            block = got[part * LANES : (part + 1) * LANES]
-            out_ref[where, 3 + part : 4 + part, :] = jnp.sum(
-                jnp.where(lo_axis == low, block, 0.0), axis=0, keepdims=True
-            )
-        out_ref[where, 7:8, :] = jnp.zeros((1, rows), F32)
-
-    def send_rows(step, carry):
-        make_rows(lax.rem(blk + step + 1, n_blk), row_src, lax.rem(blk + step + 1, n_blk))
-        row_copy(step + 1).start()
-        return carry
-
-    loop(n_blk - 1, send_rows, 0)
+        out_ref[where, 2:3, :] = ri_ref[0, 0, pl.ds(tile, 1), :].astype(F32)
+        out_ref[where, 3:8, :] = jnp.zeros((5, rows), F32)
+
+    def send_codes(step, carry):
+        tile = lax.rem(blk + step + 1, n_blk)
+        make_codes(tile, code_src, tile)
+        code_copy(step + 1).start()
+        return carry
+
+    loop(n_blk - 1, send_codes, 0)
+    make_codes(blk, code_buf, blk)
+
+    tile_rows = slots * n_ch
+    for part in range(4):
+        full = jnp.concatenate(masked[part], axis=0)
+        tall = jnp.concatenate(
+            [full[:, cut * LANES : (cut + 1) * LANES] for cut in range(cuts)], axis=0
+        )
+        data_t[part * LANES : (part + 1) * LANES, :] = tall.T.astype(BF16)
 
     for copy in rs_copies:
         copy.wait_recv()
@@ -226,6 +253,29 @@
 
     lax.fori_loop(1, n_dev, ag_start, 0)
 
+    hi_axis = iota((tile_rows * cuts, rows), 0)
+    lo_axis = iota((LANES, rows), 0)
+
+    def make_rows(tile, out_ref, where):
+        place = ri_ref[0, 0, pl.ds(tile, 1), :]
+        high = ((place // LANES) % cuts) * tile_rows + place // n_base
+        high = jnp.where(place < 0, -1, high)
+        low = jnp.where(place < 0, 0, place) % LANES
+        pick = jnp.where(hi_axis == high, 1.0, 0.0).astype(BF16)
+        got = dot(data_t[...], pick)
+        for part in range(4):
+            block = got[part * LANES : (part + 1) * LANES]
+            out_ref[where, part : part + 1, :] = jnp.sum(
+                jnp.where(lo_axis == low, block, 0.0), axis=0, keepdims=True
+            )
+
+    def send_rows(step, carry):
+        tile = lax.rem(blk + step + 1, n_blk)
+        make_rows(tile, row_src, tile)
+        row_copy(step + 1).start()
+        return carry
+
+    loop(n_blk - 1, send_rows, 0)
     make_rows(blk, row_buf, blk)
 
     el = iota((LANES, n_base), 0) % side
@@ -241,11 +291,11 @@
     gain_real = amp * jnp.cos(phase)
     gain_imag = amp * jnp.sin(phase)
 
-    def row_wait(step, carry):
-        row_copy(step + 1).wait_recv()
-        return carry
-
-    loop(n_blk - 1, row_wait, 0)
+    def code_wait(step, carry):
+        code_copy(step + 1).wait_recv()
+        return carry
+
+    loop(n_blk - 1, code_wait, 0)
 
     cell = iota((TS, LANES), 0)
     turn = (cell % (2 * KS)).astype(F32) * (math.pi / KS)
@@ -262,9 +312,9 @@
         return jnp.where(inside, wave * wave, 0.0).astype(BF16)
 
     def prepare(k, carry):
-        ku_buf[k] = taper(row_buf[k, 0:1, :])
-        kv_buf[k] = taper(row_buf[k, 1:2, :])
-        place = row_buf[k, 2:3, :].astype(jnp.int32)
+        ku_buf[k] = taper(code_buf[k, 0:1, :])
+        kv_buf[k] = taper(code_buf[k, 1:2, :])
+        place = code_buf[k, 2:3, :].astype(jnp.int32)
         place = jnp.where(place < 0, 0, place)
         pa_buf[k] = jnp.where(lane_side == (place // side) % side, 1.0, 0.0).astype(BF16)
         pb_buf[k] = jnp.where(lane_side == place % side, 1.0, 0.0).astype(BF16)
@@ -344,8 +394,9 @@
             ),
             axis=0,
         )
-        hi, mid, low = split3(terms)
-        folded = dot(hi, fold_ab[...]) + dot(mid, fold_ab[...]) + dot(low, fold_ab[...])
+        folded = dot(jnp.concatenate(split3(terms), axis=0), fold_ab[...])
+        count = 6 * pairs
+        folded = folded[:count] + folded[count : 2 * count] + folded[2 * count :]
         num_real, num_imag, den = (
             placed(
                 folded[c * pairs : (c + 1) * pairs, :LANES],
@@ -369,8 +420,14 @@
     table_b = pieces(gain_real, gain_imag, mask_b)
     pair_axis = iota((pairs, rows), 0)
 
+    def row_wait(step, carry):
+        row_copy(step + 1).wait_recv()
+        return carry
+
+    loop(n_blk - 1, row_wait, 0)
+
     def grid_rows(k, acc):
-        place = row_buf[k, 2:3, :].astype(jnp.int32)
+        place = code_buf[k, 2:3, :].astype(jnp.int32)
         pair = (jnp.where(place < 0, 0, place) // (n_ch * n_base)) * n_blk + k
         hit = pair_axis == pair
 
@@ -379,8 +436,8 @@
 
         ar, ai = (pick(x) for x in joined(dot(table_a, pa_buf[k])))
         br, bi = (pick(x) for x in joined(dot(table_b, pb_buf[k])))
-        vr, vi = row_buf[k, 3:4, :], row_buf[k, 4:5, :]
-        mr, mi = row_buf[k, 5:6, :], row_buf[k, 6:7, :]
+        vr, vi = row_buf[k, 0:1, :], row_buf[k, 1:2, :]
+        mr, mi = row_buf[k, 2:3, :], row_buf[k, 3:4, :]
         tr = mr * br + mi * bi
         ti = mi * br - mr * bi
         live = place >= 0
@@ -406,10 +463,22 @@
     lax.fori_loop(1, n_dev, ag_done, 0)
 
     def row_done(step, carry):
+        code_copy(step + 1).wait_send()
         row_copy(step + 1).wait_send()
         return carry
 
     loop(n_blk - 1, row_done, 0)
+
+
+def store(grid_in, gains_in, grid_out, gains_out, sem):
+    copies = (
+        pltpu.make_async_copy(grid_in, grid_out, sem.at[0]),
+        pltpu.make_async_copy(gains_in, gains_out, sem.at[1]),
+    )
+    for copy in copies:
+        copy.start()
+    for copy in copies:
+        copy.wait()
 
 
 def shards(
@@ -421,15 +490,30 @@
     n_dev = n_blk * n_chan
     piece = n_base // LANES // n_chan * 8
     dma = pltpu.SemaphoreType.DMA
-    return pl.pallas_call(
+    inputs = (
+        pair_map,
+        visibilities,
+        model_vis,
+        flag_mask,
+        gain_amp.reshape(1, stations),
+        gain_phase.reshape(1, stations),
+        row_index,
+        cell_codes,
+    )
+    inputs = tuple(pltpu.with_memory_space_constraint(x, pltpu.HBM) for x in inputs)
+    vmem = pl.BlockSpec(memory_space=pltpu.VMEM)
+    hbm = pl.BlockSpec(memory_space=pltpu.HBM)
+    out_shape = (
+        jax.ShapeDtypeStruct((1, 1, 2, TS, TS), F32),
+        jax.ShapeDtypeStruct((2, stations), F32),
+    )
+    results = pl.pallas_call(
         functools.partial(kernel, n_blk, n_chan),
-        out_shape=(
-            jax.ShapeDtypeStruct((1, 1, 2, TS, TS), F32),
-            jax.ShapeDtypeStruct((2, stations), F32),
-        ),
-        in_specs=[pl.BlockSpec(memory_space=pltpu.VMEM)] * 8,
-        out_specs=(pl.BlockSpec(memory_space=pltpu.VMEM),) * 2,
-        scratch_shapes=[
+        out_shape=out_shape,
+        in_specs=[hbm] * 8,
+        out_specs=(vmem, vmem),
+        scratch_shapes=[pltpu.VMEM(x.shape, x.dtype) for x in inputs]
+        + [
             pltpu.VMEM((n_chan, piece, LANES), F32),
             pltpu.VMEM((n_chan, piece, LANES), F32),
             pltpu.VMEM((piece, LANES), F32),
@@ -437,6 +521,8 @@
             pltpu.VMEM((4 * LANES, slots * n_ch * n_base // LANES), BF16),
             pltpu.VMEM((n_blk, 8, rows), F32),
             pltpu.VMEM((n_blk, 8, rows), F32),
+            pltpu.VMEM((n_blk, 4, rows), F32),
+            pltpu.VMEM((n_blk, 4, rows), F32),
             pltpu.VMEM((n_blk, TS, rows), BF16),
             pltpu.VMEM((n_blk, TS, rows), BF16),
             pltpu.VMEM((n_blk, LANES, rows), BF16),
@@ -450,21 +536,26 @@
             dma((n_dev,)),
             dma((n_blk,)),
             dma((n_blk,)),
+            dma((n_blk,)),
+            dma((n_blk,)),
+            dma((8,)),
         ],
         compiler_params=pltpu.CompilerParams(
-            collective_id=0, has_side_effects=True, vmem_limit_bytes=56 * 1024 * 1024
+            collective_id=0,
+            has_side_effects=True,
+            vmem_limit_bytes=(12 + n_blk * 11 // 16) * 1024 * 1024,
         ),
         name="solve_and_grid",
-    )(
-        pair_map,
-        visibilities,
-        model_vis,
-        flag_mask,
-        gain_amp.reshape(1, stations),
-        gain_phase.reshape(1, stations),
-        row_index,
-        cell_codes,
-    )
+    )(*inputs)
+    return pl.pallas_call(
+        store,
+        out_shape=out_shape,
+        in_specs=[vmem] * 2,
+        out_specs=(hbm, hbm),
+        scratch_shapes=[dma((2,))],
+        compiler_params=pltpu.CompilerParams(vmem_limit_bytes=1024 * 1024),
+        name="store",
+    )(*results)
 
 
 def solution(mesh):

time: 24.7 us -> 21.7 us (0.88)
  local copies, waits for them, and re-layouts: 2.17 us -> 0 us
  Pallas kernels: 21.6 us -> 20.8 us
    unnamed x4 -> x0, local copies, waits for them, and re-layouts: 2.17 us -> none
    pallas_call x1 -> x2, Pallas kernels: 21.6 us -> 20.8 us  [the longest x1 20.1 us: shards(): pl.pallas_call(functools.partial(kernel, n_blk, n_chan), out_shape=out_sh...]
where the time goes in v2:
time: 21.7 us; the launch traced here: 21.4 us
  Pallas kernels  20.8 us (96%)
  between operations  0.64 us (3%)
    pallas_call x1, Pallas kernels, shards(): pl.pallas_call(functools.partial(kernel, n_blk, n_chan), out_shape=out_sh...  20.1 us
    pallas_call x1, Pallas kernels, shards(): pl.pallas_call(store, out_shape=out_shape, in_specs=[vmem] * 2, out_specs...  0.68 us

profile of v2, /device:TPU:0, one launch (start us, length us, event | category | flops | bytes accessed | tf_op | source)
XLA Modules:
  0.0 21.4 jit_solution(9668856942849617772)
XLA Ops:
  0.6 20.1 %solve_and_grid.1 = (f32[1,1,2,128,128]{4,3,2,1,0:T(8,128)S(1)}, f32[2,512]{1,0:T(2,128)S(1)}) custom-call(s32[2,2]{1,0:T(2,128)} %pm_hbm.1, bf16[2,2,16,1024]{3,2,1,0:T(8,128)(2,1)} %vis_hbm.1, bf16[2,2,16,1024]{3,2,1,0:T(8,128)(2,1)} %mod_hbm.1, s32[2,16,1024]{2,1,0:T(8,128)} %flag_hbm.1, f32[1,512]{1,0:T(1,128)} %bitcast.2, f32[1,512]{1,0:T(1,128)} %bitcast.3, ...), custom_call_target="tpu_custom_call" | custom-call | tf_op jit(solution)/shard_map/solve_and_grid/pallas_call | solution.py:510
  20.8 0.7 %store.1 = (f32[1,1,2,128,128]{4,3,2,1,0:T(8,128)}, f32[2,512]{1,0:T(2,128)}) custom-call(f32[1,1,2,128,128]{4,3,2,1,0:T(8,128)S(1)} %get-tuple-element.4.grid_in, f32[2,512]{1,0:T(2,128)S(1)} %get-tuple-element.5.gains_in), custom_call_target="tpu_custom_call" | custom-call | tf_op jit(solution)/shard_map/store/pallas_call | solution.py:550

commit v3 on v2

--- a/solution.py
+++ b/solution.py
@@ -223,6 +223,30 @@
         )
         data_t[part * LANES : (part + 1) * LANES, :] = tall.T.astype(BF16)
 
+    hi_axis = iota((tile_rows * cuts, rows), 0)
+    lo_axis = iota((LANES, rows), 0)
+
+    def make_rows(tile, out_ref, where):
+        place = ri_ref[0, 0, pl.ds(tile, 1), :]
+        high = ((place // LANES) % cuts) * tile_rows + place // n_base
+        high = jnp.where(place < 0, -1, high)
+        low = jnp.where(place < 0, 0, place) % LANES
+        pick = jnp.where(hi_axis == high, 1.0, 0.0).astype(BF16)
+        got = dot(data_t[...], pick)
+        for part in range(4):
+            block = got[part * LANES : (part + 1) * LANES]
+            out_ref[where, part : part + 1, :] = jnp.sum(
+                jnp.where(lo_axis == low, block, 0.0), axis=0, keepdims=True
+            )
+
+    def send_rows(step, carry):
+        tile = lax.rem(blk + step + 1, n_blk)
+        make_rows(tile, row_src, tile)
+        row_copy(step + 1).start()
+        return carry
+
+    loop(n_blk - 1, send_rows, 0)
+
     for copy in rs_copies:
         copy.wait_recv()
     total = rs_src[chan]
@@ -253,31 +277,7 @@
 
     lax.fori_loop(1, n_dev, ag_start, 0)
 
-    hi_axis = iota((tile_rows * cuts, rows), 0)
-    lo_axis = iota((LANES, rows), 0)
-
-    def make_rows(tile, out_ref, where):
-        place = ri_ref[0, 0, pl.ds(tile, 1), :]
-        high = ((place // LANES) % cuts) * tile_rows + place // n_base
-        high = jnp.where(place < 0, -1, high)
-        low = jnp.where(place < 0, 0, place) % LANES
-        pick = jnp.where(hi_axis == high, 1.0, 0.0).astype(BF16)
-        got = dot(data_t[...], pick)
-        for part in range(4):
-            block = got[part * LANES : (part + 1) * LANES]
-            out_ref[where, part : part + 1, :] = jnp.sum(
-                jnp.where(lo_axis == low, block, 0.0), axis=0, keepdims=True
-            )
-
-    def send_rows(step, carry):
-        tile = lax.rem(blk + step + 1, n_blk)
-        make_rows(tile, row_src, tile)
-        row_copy(step + 1).start()
-        return carry
-
-    loop(n_blk - 1, send_rows, 0)
     make_rows(blk, row_buf, blk)
-
     el = iota((LANES, n_base), 0) % side
     et = iota((LANES, n_base), 1)
     ex_a[...] = jnp.where(el == et // side, 1.0, 0.0).astype(BF16)
@@ -394,9 +394,9 @@
             ),
             axis=0,
         )
-        folded = dot(jnp.concatenate(split3(terms), axis=0), fold_ab[...])
+        folded = dot(jnp.concatenate(split3(terms)[:2], axis=0), fold_ab[...])
         count = 6 * pairs
-        folded = folded[:count] + folded[count : 2 * count] + folded[2 * count :]
+        folded = folded[:count] + folded[count : 2 * count]
         num_real, num_imag, den = (
             placed(
                 folded[c * pairs : (c + 1) * pairs, :LANES],

time: 21.7 us -> 20.9 us (0.963)
  Pallas kernels: 20.8 us -> 20 us
    pallas_call x1, Pallas kernels: 20.1 us -> 19.3 us  [shards(): pl.pallas_call(functools.partial(kernel, n_blk, n_chan), out_shape=out_sh...]
where the time goes in v3:
time: 20.9 us; the launch traced here: 20.6 us
  Pallas kernels  20 us (96%)
  between operations  0.64 us (3%)
    pallas_call x1, Pallas kernels, shards(): pl.pallas_call(functools.partial(kernel, n_blk, n_chan), out_shape=out_sh...  19.3 us
    pallas_call x1, Pallas kernels, shards(): pl.pallas_call(store, out_shape=out_shape, in_specs=[vmem] * 2, out_specs...  0.68 us

profile of v3, /device:TPU:0, one launch (start us, length us, event | category | flops | bytes accessed | tf_op | source)
XLA Modules:
  0.0 20.6 jit_solution(14729999842778482986)
XLA Ops:
  0.6 19.3 %solve_and_grid.1 = (f32[1,1,2,128,128]{4,3,2,1,0:T(8,128)S(1)}, f32[2,512]{1,0:T(2,128)S(1)}) custom-call(s32[2,2]{1,0:T(2,128)} %pm_hbm.1, bf16[2,2,16,1024]{3,2,1,0:T(8,128)(2,1)} %vis_hbm.1, bf16[2,2,16,1024]{3,2,1,0:T(8,128)(2,1)} %mod_hbm.1, s32[2,16,1024]{2,1,0:T(8,128)} %flag_hbm.1, f32[1,512]{1,0:T(1,128)} %bitcast.2, f32[1,512]{1,0:T(1,128)} %bitcast.3, ...), custom_call_target="tpu_custom_call" | custom-call | tf_op jit(solution)/shard_map/solve_and_grid/pallas_call | solution.py:510
  20.0 0.7 %store.1 = (f32[1,1,2,128,128]{4,3,2,1,0:T(8,128)}, f32[2,512]{1,0:T(2,128)}) custom-call(f32[1,1,2,128,128]{4,3,2,1,0:T(8,128)S(1)} %get-tuple-element.4.grid_in, f32[2,512]{1,0:T(2,128)S(1)} %get-tuple-element.5.gains_in), custom_call_target="tpu_custom_call" | custom-call | tf_op jit(solution)/shard_map/store/pallas_call | solution.py:550
